TPU v7x, 32 devices: a whole 2x2x4 slice. The times are simulated.
32 devices in a mesh: dp: 8 (over z, x), mp: 4 (over y, core).
Axes of the slice: x: 2, y: 2, z: 4, core: 2. Of those that a mesh axis runs over, the one named last changes fastest.
Arguments:
- query_emb: bfloat16 [2048, 768], P('dp'), may hold values from -6 to 6
- positive_list: int32 [2048], replicated, may hold values from 0 to 32767
- centroids: float32 [32768, 768], P(('dp', 'mp')), may hold values from -0.6 to 0.6
- first_moment: float32 [32768, 768], P(('dp', 'mp')), may hold values from -3 to 3
- second_moment: float32 [32768, 768], P(('dp', 'mp')), may hold values from 0.05 to 2
Outputs:
- new_centroids: float32 [32768, 768], P(('dp', 'mp'))
- new_first: float32 [32768, 768], P(('dp', 'mp'))
- new_second: float32 [32768, 768], P(('dp', 'mp'))
- mean_loss: float32 [], replicated
All inputs are finite; a program needn't handle non-finite values.
Results may differ from a plain program's by a relative error of at most 0.00097.
Values may be sent and summed in bfloat16 or wider, within the bound.
A program may use at most 64 MiB of HBM per device.

v0:
```python
import jax
import jax.numpy as jnp
from jax import lax
from jax.sharding import PartitionSpec as P

beta_first = 0.9
beta_second = 0.95
learn_rate = 0.01
epsilon = 1e-08


def adam_update(centroids, first_moment, second_moment, gradient):
    new_first = beta_first * first_moment + (1.0 - beta_first) * gradient
    new_second = beta_second * second_moment + (1.0 - beta_second) * gradient * gradient
    new_centroids = centroids - learn_rate * new_first / (jnp.sqrt(new_second) + epsilon)
    return (new_centroids, new_first, new_second)


def target_logit(logits, is_target):
    return jnp.sum(jnp.where(is_target, logits, jnp.zeros_like(logits)), axis=1)


def row_terms(logits, is_target, row_peak, row_mass, row_target):
    log_norm = row_peak + jnp.log(row_mass)
    row_loss = log_norm - row_target
    weights = (jnp.exp(logits - log_norm[:, None]) - is_target.astype(jnp.float32)).astype(
        jnp.bfloat16
    )
    return (row_loss, weights)


def shards(query_emb, positive_list, centroids, first_moment, second_moment):
    table_half = centroids.astype(jnp.bfloat16)
    own_lists = centroids.shape[0]
    count_mp = lax.axis_size("mp")
    dp_index = lax.axis_index("dp")
    mp_index = lax.axis_index("mp")
    gathered = lax.all_gather(query_emb, "dp", axis=0, tiled=True)
    logits = jnp.einsum("rd,kd->rk", gathered, table_half, preferred_element_type=jnp.float32)
    shard_block = dp_index * count_mp + mp_index
    global_col = shard_block * own_lists + lax.iota(jnp.int32, own_lists)
    is_target = global_col[None, :] == positive_list[:, None]
    row_peak = lax.pmax(jnp.max(logits, axis=1).astype(jnp.bfloat16), ("dp", "mp")).astype(
        jnp.float32
    )
    local_mass = jnp.sum(jnp.exp(logits - row_peak[:, None]), axis=1)
    row_mass, row_target = lax.psum((local_mass, target_logit(logits, is_target)), ("dp", "mp"))
    row_loss, weights = row_terms(logits, is_target, row_peak, row_mass, row_target)
    mean_loss = jnp.mean(row_loss)
    gradient = jnp.einsum("rk,rd->kd", weights, gathered, preferred_element_type=jnp.float32)
    new_centroids, new_first, new_second = adam_update(
        centroids, first_moment, second_moment, gradient
    )
    return (new_centroids, new_first, new_second, mean_loss)


def solution(mesh):
    in_specs = (
        P("dp", None),
        P(),
        P(("dp", "mp"), None),
        P(("dp", "mp"), None),
        P(("dp", "mp"), None),
    )
    out_specs = (P(("dp", "mp"), None), P(("dp", "mp"), None), P(("dp", "mp"), None), P())
    return jax.shard_map(shards, mesh=mesh, in_specs=in_specs, out_specs=out_specs, check_vma=False)
```

profile of v0, /device:TPU:0, one launch (start us, length us, event | category | flops | bytes accessed | tf_op | source)
XLA Modules:
  0.0 188.3 jit_solution(12831864654990041094)
XLA Ops:
  7.2 0.0 all-gather.2.cloned.1.call-start
  7.2 0.7 all-gather.2.cloned.1.call-update
  7.9 0.0 copy-start
  7.9 65.0 %all-gather.2.cloned.1.call-done = bf16[2048,768]{1,0:T(8,128)(2,1)} async-done(((bf16[256,768]{1,0:T(8,128)(2,1)}), bf16[2048,768]{1,0:T(8,128)(2,1)}) %all-gather.2.cloned.1.call-update) | async-done | bytes 3145744 | tf_op jit(solution)/shard_map/all_gather | solution.py:38
  72.9 9.5 %fusion.12 = (bf16[2048]{0:T(1024)(128)(2,1)S(1)}, f32[2048,1024]{0,1:T(8,128)}) fusion(bf16[2048,768]{1,0:T(8,128)(2,1)} %all-gather.2.cloned.1.call-done, f32[1024,768]{1,0:T(8,128)} %param.7), kind=kOutput, calls=%fused_computation.19 | convolution fusion | flops 3224107008 | bytes 14684160 | tf_op jit(solution)/shard_map/rd,kd->rk/dot_general | solution.py:39
  82.4 39.2 %pmax.7 = bf16[2048]{0:T(1024)(128)(2,1)S(1)} all-reduce(bf16[2048]{0:T(1024)(128)(2,1)S(1)} %get-tuple-element.13), channel_id=1, replica_groups=mesh['dp'=8,'mp'=4] {'dp','mp'}, use_global_device_ids=true, to_apply=%region_1.0 | all-reduce | flops 2048 | bytes 8192 | tf_op jit(solution)/shard_map/pmax | solution.py:43
  121.7 0.0 copy-done
  121.7 0.0 copy-start.1
  121.7 4.7 %fusion.2 = (f32[2048]{0:T(1024)S(1)}, f32[2048]{0:T(1024)S(1)}) fusion(f32[2048,1024]{0,1:T(8,128)} %get-tuple-element.14, s32[2048]{0:T(1024)S(1)} %copy-done, s32[1024]{0:T(1024)S(1)} %iota_add_fusion, f32[2048]{0:T(1024)S(1)} %convert_element_type.17), kind=kLoop, calls=%fused_computation.4 | loop fusion | flops 10481664 | bytes 8425472 | tf_op jit(solution)/shard_map/reduce_sum | solution.py:20
  126.4 40.0 %all-reduce = (f32[2048]{0:T(1024)S(1)}, f32[2048]{0:T(1024)S(1)}) all-reduce(f32[2048]{0:T(1024)S(1)} %get-tuple-element.5, f32[2048]{0:T(1024)S(1)} %get-tuple-element.4), channel_id=1, replica_groups=mesh['dp'=8,'mp'=4] {'dp','mp'}, use_global_device_ids=true, to_apply=%region_3.4 | all-reduce | flops 4096 | bytes 32768 | tf_op jit(solution)/shard_map/psum | solution.py:47
  166.5 0.6 subtract_reduce_fusion
  167.8 0.0 copy-done.1
  167.8 12.5 %divide_subtract_fusion = (f32[1024,768]{1,0:T(8,128)}, f32[1024,768]{1,0:T(8,128)}, f32[1024,768]{1,0:T(8,128)}) fusion(f32[1024,768]{1,0:T(8,128)S(1)} %copy-done.1, f32[1024,768]{1,0:T(8,128)} %param.8, f32[1024,768]{1,0:T(8,128)} %param.9, bf16[2048,768]{1,0:T(8,128)(2,1)} %all-gather.2.cloned.1.call-done, f32[2048,1024]{0,1:T(8,128)} %get-tuple-element.14, ...), kind=kOutput, calls=%fused_computation.12 | convolution fusion | flops 3240361984 | bytes 30429184 | tf_op jit(solution)/shard_map/rk,rd->kd/dot_general | solution.py:50
  (2 shorter events, 0.0 us)
Async XLA Ops:
  7.2 65.8 %all-gather.2.cloned.1.call-start = ((), (), s32[]{:S(2)}) async-start(), calls=%async_computation | async-start | bytes 3538944 | tf_op jit(solution)/shard_map/all_gather | solution.py:38
  7.9 113.8 %copy-start = (s32[2048]{0:T(1024)S(1)}, s32[2048]{0:T(1024)}, u32[]{:S(2)}) copy-start(s32[2048]{0:T(1024)} %param.6) | copy-start | bytes 24580
  121.7 46.1 %copy-start.1 = (f32[1024,768]{1,0:T(8,128)S(1)}, f32[1024,768]{1,0:T(8,128)}, u32[]{:S(2)}) copy-start(f32[1024,768]{1,0:T(8,128)} %param.7) | copy-start | bytes 9437188
Sparse Core Ops, SparseCore 0:
  10.2 62.7 all-gather.1
where the time goes:
time: 189 us; the launch traced here: 188 us
  blocking collectives  79.3 us (42%)
  waiting for transfers between devices  65.7 us (35%)
  matrix products  22.1 us (12%)
  between operations  15.8 us (8%)
  other arithmetic  5.35 us (3%)
    all_gather x1, waiting for transfers between devices, shards(): gathered = lax.all_gather(query_emb, 'dp', axis=0, tiled=True)  65 us
    psum x1, blocking collectives, shards(): lax.psum((local_mass, target_logit(logits, is_target)), ('dp', 'mp'))  40 us
    pmax x1, blocking collectives, shards(): lax.pmax(jnp.max(logits, axis=1).astype(jnp.bfloat16), ('dp', 'mp'))  39.2 us
    dot_general x1, matrix products, shards(): jnp.einsum('rk,rd->kd', weights, gathered, preferred_element_type=jnp.flo...  12.5 us
    dot_general x1, matrix products, shards(): jnp.einsum('rd,kd->rk', gathered, table_half, preferred_element_type=jnp....  9.52 us
    reduce_sum x1, other arithmetic, target_logit(): return jnp.sum(jnp.where(is_target, logits, jnp.zeros_like(logits)), axis=1)  4.74 us
  transfers between devices with their start and end apart: 1, of which 1 were waited for; matrix products, arithmetic and copies ran while one was open for 0% of the time, Pallas kernels for 0%

commit v1 on v0

--- a/solution.py
+++ b/solution.py
@@ -44,7 +44,9 @@
         jnp.float32
     )
     local_mass = jnp.sum(jnp.exp(logits - row_peak[:, None]), axis=1)
-    row_mass, row_target = lax.psum((local_mass, target_logit(logits, is_target)), ("dp", "mp"))
+    row_mass, row_target = lax.psum(
+        lax.psum((local_mass, target_logit(logits, is_target)), "mp"), "dp"
+    )
     row_loss, weights = row_terms(logits, is_target, row_peak, row_mass, row_target)
     mean_loss = jnp.mean(row_loss)
     gradient = jnp.einsum("rk,rd->kd", weights, gathered, preferred_element_type=jnp.float32)

time: 189 us -> 195 us (1.032)
  blocking collectives: 79.3 us -> 85.9 us
    psum x1 -> x2, blocking collectives: 40 us -> 46.7 us  [the longest x1 35.8 us: shards(): lax.psum(lax.psum((local_mass, target_logit(logits, is_target)), 'mp'), '...]
where the time goes in v1:
time: 195 us
  blocking collectives  85.9 us (44%)
  waiting for transfers between devices  65.7 us (34%)
  matrix products  22.1 us (11%)
  between operations  15.8 us (8%)
  other arithmetic  5.36 us (3%)
    all_gather x1, waiting for transfers between devices, shards(): gathered = lax.all_gather(query_emb, 'dp', axis=0, tiled=True)  65 us
    pmax x1, blocking collectives, shards(): lax.pmax(jnp.max(logits, axis=1).astype(jnp.bfloat16), ('dp', 'mp'))  39.2 us
    psum x1, blocking collectives, shards(): lax.psum(lax.psum((local_mass, target_logit(logits, is_target)), 'mp'), '...  35.8 us
    dot_general x1, matrix products, shards(): jnp.einsum('rk,rd->kd', weights, gathered, preferred_element_type=jnp.flo...  12.5 us
    psum x1, blocking collectives, shards(): lax.psum((local_mass, target_logit(logits, is_target)), 'mp')  10.9 us
    dot_general x1, matrix products, shards(): jnp.einsum('rd,kd->rk', gathered, table_half, preferred_element_type=jnp....  9.52 us
    reduce_sum x1, other arithmetic, target_logit(): return jnp.sum(jnp.where(is_target, logits, jnp.zeros_like(logits)), axis=1)  4.74 us
  transfers between devices with their start and end apart: 1, of which 1 were waited for; matrix products, arithmetic and copies ran while one was open for 0% of the time, Pallas kernels for 0%

profile of v1, /device:TPU:0, one launch (start us, length us, event | category | flops | bytes accessed | tf_op | source)
XLA Modules:
  0.0 194.9 jit_solution(18027881691983232604)
XLA Ops:
  7.2 0.0 all-gather.2.cloned.1.call-start
  7.2 0.7 all-gather.2.cloned.1.call-update
  7.9 0.0 copy-start
  7.9 65.0 %all-gather.2.cloned.1.call-done = bf16[2048,768]{1,0:T(8,128)(2,1)} async-done(((bf16[256,768]{1,0:T(8,128)(2,1)}), bf16[2048,768]{1,0:T(8,128)(2,1)}) %all-gather.2.cloned.1.call-update) | async-done | bytes 3145744 | tf_op jit(solution)/shard_map/all_gather | solution.py:38
  72.9 9.5 %fusion.12 = (bf16[2048]{0:T(1024)(128)(2,1)S(1)}, f32[2048,1024]{0,1:T(8,128)}) fusion(bf16[2048,768]{1,0:T(8,128)(2,1)} %all-gather.2.cloned.1.call-done, f32[1024,768]{1,0:T(8,128)} %param.7), kind=kOutput, calls=%fused_computation.19 | convolution fusion | flops 3224107008 | bytes 14684160 | tf_op jit(solution)/shard_map/rd,kd->rk/dot_general | solution.py:39
  82.4 39.2 %pmax.7 = bf16[2048]{0:T(1024)(128)(2,1)S(1)} all-reduce(bf16[2048]{0:T(1024)(128)(2,1)S(1)} %get-tuple-element.15), channel_id=1, replica_groups=mesh['dp'=8,'mp'=4] {'dp','mp'}, use_global_device_ids=true, to_apply=%region_1.0 | all-reduce | flops 2048 | bytes 8192 | tf_op jit(solution)/shard_map/pmax | solution.py:43
  121.7 0.0 copy-done
  121.7 0.0 copy-start.1
  121.7 4.7 %fusion.2 = (f32[2048]{0:T(1024)S(1)}, f32[2048]{0:T(1024)S(1)}) fusion(f32[2048,1024]{0,1:T(8,128)} %get-tuple-element.16, s32[2048]{0:T(1024)S(1)} %copy-done, s32[1024]{0:T(1024)S(1)} %iota_add_fusion, f32[2048]{0:T(1024)S(1)} %convert_element_type.17), kind=kLoop, calls=%fused_computation.4 | loop fusion | flops 10481664 | bytes 8425472 | tf_op jit(solution)/shard_map/reduce_sum | solution.py:20
  126.4 10.9 %all-reduce.1 = (f32[2048]{0:T(1024)S(1)}, f32[2048]{0:T(1024)S(1)}) all-reduce(f32[2048]{0:T(1024)S(1)} %get-tuple-element.5, f32[2048]{0:T(1024)S(1)} %get-tuple-element.4), channel_id=1, replica_groups=mesh['dp'=8,'mp'=4] {'mp'}, use_global_device_ids=true, to_apply=%region_3.4 | all-reduce | flops 4096 | bytes 32768 | tf_op jit(solution)/shard_map/psum | solution.py:48
  137.4 35.8 %all-reduce = (f32[2048]{0:T(1024)S(1)}, f32[2048]{0:T(1024)S(1)}) all-reduce(f32[2048]{0:T(1024)S(1)} %get-tuple-element.8, f32[2048]{0:T(1024)S(1)} %get-tuple-element.9), channel_id=1, replica_groups=mesh['dp'=8,'mp'=4] {'dp'}, use_global_device_ids=true, to_apply=%region_4.5 | all-reduce | flops 4096 | bytes 32768 | tf_op jit(solution)/shard_map/psum | solution.py:47
  173.1 0.6 subtract_reduce_fusion
  174.4 0.0 copy-done.1
  174.4 12.5 %divide_subtract_fusion = (f32[1024,768]{1,0:T(8,128)}, f32[1024,768]{1,0:T(8,128)}, f32[1024,768]{1,0:T(8,128)}) fusion(f32[1024,768]{1,0:T(8,128)S(1)} %copy-done.1, f32[1024,768]{1,0:T(8,128)} %param.8, f32[1024,768]{1,0:T(8,128)} %param.9, bf16[2048,768]{1,0:T(8,128)(2,1)} %all-gather.2.cloned.1.call-done, f32[2048,1024]{0,1:T(8,128)} %get-tuple-element.16, ...), kind=kOutput, calls=%fused_computation.12 | convolution fusion | flops 3240361984 | bytes 30429184 | tf_op jit(solution)/shard_map/rk,rd->kd/dot_general | solution.py:52
  (2 shorter events, 0.0 us)
Async XLA Ops:
  7.2 65.8 %all-gather.2.cloned.1.call-start = ((), (), s32[]{:S(2)}) async-start(), calls=%async_computation | async-start | bytes 3538944 | tf_op jit(solution)/shard_map/all_gather | solution.py:38
  7.9 113.8 %copy-start = (s32[2048]{0:T(1024)S(1)}, s32[2048]{0:T(1024)}, u32[]{:S(2)}) copy-start(s32[2048]{0:T(1024)} %param.6) | copy-start | bytes 24580
  121.7 52.7 %copy-start.1 = (f32[1024,768]{1,0:T(8,128)S(1)}, f32[1024,768]{1,0:T(8,128)}, u32[]{:S(2)}) copy-start(f32[1024,768]{1,0:T(8,128)} %param.7) | copy-start | bytes 9437188
Sparse Core Ops, SparseCore 0:
  10.2 62.7 all-gather.1
